TPU v7x, 512 devices: a whole 4x8x8 slice. The times are simulated.
512 devices in a mesh: row: 64 (over x, y, core), col: 8 (over z).
Axes of the slice: x: 4, y: 8, z: 8, core: 2. Of those that a mesh axis runs over, the one named last changes fastest.
Arguments:
- matrix: float32 [16384, 4096], P('row', 'col'), may hold values from -7.8125 to 7.8125
Outputs:
- r_top: float32 [512, 4096], P(None, 'col')
- basis: float32 [16384, 512], P('row')
All inputs are finite; a program needn't handle non-finite values.
Results may differ from a plain program's by a relative error of at most 0.0003.
Values sent between devices are 32-bit elements; how exact they have to be, the bound alone decides.
No kernel may reach another device: no remote copies, remote signals or barrier semaphores. Data moves between devices by JAX's collectives and lax.ppermute only.
A program may use at most 64 MiB of HBM per device.

v0:
```python
import math

import jax
import jax.numpy as jnp
from jax import lax
from jax.experimental import pallas as pl
from jax.experimental.pallas import tpu as pltpu
from jax.sharding import Mesh
from jax.sharding import PartitionSpec as P


PANEL = 256
WIDE = 2 * PANEL
TILE = 128
STEP = 32
ROW = ("x", "y", "core")
PLANE = ("x", "y")
HIGHEST = lax.Precision.HIGHEST


def inner(left, right):
    return lax.dot_general(
        left,
        right,
        (((0,), (0,)), ((), ())),
        precision=HIGHEST,
        preferred_element_type=jnp.float32,
    )


def product(left, right):
    return jnp.dot(left, right, precision=HIGHEST, preferred_element_type=jnp.float32)


PLACES = {
    (0, 0): (0, 0), (0, 1): (0, 1), (0, 2): (0, 2), (0, 3): (0, 3), (3, 3): (0, 4),
    (1, 1): (1, 0), (1, 2): (1, 1), (1, 3): (1, 2), (2, 2): (1, 3), (2, 3): (1, 4),
}
NARROW = 5 * TILE


def span(place):
    return slice(place * TILE, (place + 1) * TILE)


def gram_kernel(core_ref, panels_ref, keep_ref, send_ref):
    for i in range(4):
        line = inner(panels_ref[:, span(i)], panels_ref[:, i * TILE :])
        half = PLACES[i, i][0]

        def put(ref):
            for j in range(i, 4):
                block = line[:, span(j - i)]
                ref[:, :, span(PLACES[i, j][1])] = block.reshape(*ref.shape[:2], TILE)

        @pl.when(core_ref[0] == half)
        def _():
            put(keep_ref)

        @pl.when(core_ref[0] != half)
        def _():
            put(send_ref)


def start_kernel(core_ref, own_ref, other_ref, out_ref):
    for half in range(2):

        def take(ref):
            for (i, j), (where, place) in PLACES.items():
                if where == half:
                    out_ref[span(i), span(j)] = ref[:, :, span(place)].reshape(TILE, TILE)

        @pl.when(core_ref[0] == half)
        def _():
            take(own_ref)

        @pl.when(core_ref[0] != half)
        def _():
            take(other_ref)

    factor_tiles(out_ref, 0, 1)


def finish_kernel(state_ref, out_ref):
    out_ref[...] = state_ref[...]
    factor_tiles(out_ref, 1, 4)
    row = lax.broadcasted_iota(jnp.int32, (WIDE, WIDE), 0)
    col = lax.broadcasted_iota(jnp.int32, (WIDE, WIDE), 1)
    out_ref[...] = jnp.where(col <= row, out_ref[...], 0.0)


def factor_tiles(out_ref, begin, end):
    row8 = lax.broadcasted_iota(jnp.int32, (8, TILE), 0)
    lane = lax.broadcasted_iota(jnp.int32, (8, TILE), 1)
    tiles, groups = WIDE // TILE, STEP // 8

    def outer(t, _):
        base = pl.multiple_of(t * TILE, TILE)
        for u in range(TILE // STEP):
            first = pl.multiple_of(base + u * STEP, STEP)
            block = out_ref[pl.ds(first, STEP), pl.ds(base, TILE)]
            cols = []
            for q in range(STEP):
                spread = jnp.broadcast_to(block[:, u * STEP + q : u * STEP + q + 1], (STEP, TILE))
                cols.append([spread[8 * v : 8 * v + 8] for v in range(groups)])
            rows = []
            for v in range(groups):
                rows.append([])
                for w in range(tiles):
                    values = out_ref[pl.ds(first + 8 * v, 8), TILE * w : TILE * (w + 1)]
                    here = (lane >= u * STEP) & (lane < (u + 1) * STEP) & (t == w)
                    unit = jnp.where(lane - u * STEP == row8 + 8 * v, 1.0, 0.0)
                    rows[v].append(jnp.where(here, unit, values))
            pivots = [None] * groups
            for k in range(STEP):
                vk, sk = k // 8, k % 8
                pivot = jnp.broadcast_to(cols[k][vk][sk : sk + 1], (8, TILE))
                inverse = 1.0 / pivot
                pivots[vk] = pivot if sk == 0 else jnp.where(row8 == sk, pivot, pivots[vk])
                scaled = {}
                for v in range(vk, groups):
                    s = cols[k][v] * inverse
                    scaled[v] = jnp.where(row8 > sk, s, 0.0) if v == vk else s
                for j in range(k + 1, STEP):
                    other = jnp.broadcast_to(cols[k][j // 8][j % 8 : j % 8 + 1], (8, TILE))
                    for v in range(j // 8, groups):
                        cols[j][v] = cols[j][v] - scaled[v] * other
                for w in range(tiles):
                    other = jnp.broadcast_to(rows[vk][w][sk : sk + 1], (8, TILE))
                    for v in range(vk, groups):
                        rows[v][w] = rows[v][w] - scaled[v] * other
            for v in range(groups):
                scale = lax.rsqrt(pivots[v])
                for w in range(tiles):
                    out_ref[pl.ds(first + 8 * v, 8), TILE * w : TILE * (w + 1)] = rows[v][w] * scale
            if u < TILE // STEP - 1:
                rest = TILE - (u + 1) * STEP
                done = out_ref[pl.ds(first, STEP), :]
                left = out_ref[pl.ds(first, STEP), pl.ds(base, TILE)][:, (u + 1) * STEP :]
                old = out_ref[pl.ds(first + STEP, rest), :]
                col = lax.broadcasted_iota(jnp.int32, (rest, WIDE), 1)
                old = jnp.where((col >= first) & (col < first + STEP), 0.0, old)
                out_ref[pl.ds(first + STEP, rest), :] = old - inner(left, done)

        done = out_ref[pl.ds(base, TILE), :]
        row = lax.broadcasted_iota(jnp.int32, (TILE, WIDE), 0) + base
        col = lax.broadcasted_iota(jnp.int32, (TILE, WIDE), 1)
        done = jnp.where((col <= row) | (col >= base + TILE), done, 0.0)

        def below(i, _):
            start = pl.multiple_of(i * TILE, TILE)
            old = out_ref[pl.ds(start, TILE), :]
            old = jnp.where((col >= base) & (col < base + TILE), 0.0, old)
            out_ref[pl.ds(start, TILE), :] = old - inner(
                out_ref[pl.ds(base, TILE), pl.ds(start, TILE)], done
            )
            return 0

        lax.fori_loop(t + 1, tiles, below, 0)
        return 0

    lax.fori_loop(begin, end, outer, 0)


def call(kernel, operands, shapes, flops):
    vmem, smem = pl.BlockSpec(memory_space=pltpu.VMEM), pl.BlockSpec(memory_space=pltpu.SMEM)
    return pl.pallas_call(
        kernel,
        out_shape=[jax.ShapeDtypeStruct(shape, jnp.float32) for shape in shapes],
        in_specs=[smem if a.ndim == 1 else vmem for a in operands],
        out_specs=[vmem for _ in shapes],
        compiler_params=pltpu.CompilerParams(vmem_limit_bytes=16 * 2**20),
        cost_estimate=pl.CostEstimate(flops=flops, bytes_accessed=2**21, transcendentals=0),
    )(*operands)


def exchange(blocks, axis):
    return lax.all_to_all(blocks, axis, 0, 0, tiled=True)


def spread(array, count):
    return jnp.broadcast_to(array[None], (count, *array.shape))


def swapped(array):
    return lax.ppermute(array, "core", [(0, 1), (1, 0)])


def steps(matrix):
    rows_all = matrix.shape[0] * lax.axis_size(ROW)
    chips = lax.axis_size(PLANE)
    core = lax.axis_index("core")
    which = core.reshape(1)
    col = lax.axis_index("col")

    up = lax.ppermute(matrix, "col", [(0, 3)])
    down = lax.ppermute(matrix, "col", [(0, 5)])
    keep, send = call(gram_kernel, (which, matrix), [(chips, TILE // chips, NARROW)] * 2, 600_000_000)
    half = keep + swapped(send)
    gram_part = exchange(half, PLANE)
    panels = jnp.where(col == 0, matrix, up + down)
    up = lax.ppermute(panels, "col", [(0, 1), (3, 4), (5, 6)])
    down = lax.ppermute(panels, "col", [(0, 7), (3, 2)])
    gram_part = gram_part.sum(axis=0)
    copies = [
        lax.ppermute(gram_part, "col", [(0, k)]) for k in range(1, lax.axis_size("col"))
    ]
    gram_part = jnp.where(col == 0, gram_part, sum(copies))
    own = exchange(spread(gram_part, chips), PLANE)
    panels = jnp.where((col == 0) | (col == 3) | (col == 5), panels, up + down)
    panels = lax.optimization_barrier(panels)
    products = inner(panels, matrix).reshape(2, -1, WIDE)
    mine = jnp.where(core == 0, products[0], products[1])
    half = mine + swapped(jnp.where(core == 0, products[1], products[0]))
    half, own = lax.optimization_barrier((half, own))
    part = exchange(half.reshape(chips, -1, WIDE), PLANE)
    (state,) = call(start_kernel, (which, own, swapped(own)), [(WIDE, WIDE)], 1_000_000_000)
    part, state = lax.optimization_barrier((part, state))
    half = exchange(spread(part.sum(axis=0), chips), PLANE).reshape(-1, WIDE)
    (inverse,) = call(finish_kernel, (state,), [(WIDE, WIDE)], 1_000_000_000)
    basis = product(panels, inverse.T) * math.sqrt(rows_all)
    half, basis = lax.optimization_barrier((half, basis))
    first, second = inverse[:, :PANEL], inverse[:, PANEL:]
    there = swapped(half)
    top = product(jnp.where(core == 0, first, second), half)
    top = top + product(jnp.where(core == 0, second, first), there)
    row = lax.broadcasted_iota(jnp.int32, (WIDE, WIDE), 0)
    column = lax.broadcasted_iota(jnp.int32, (WIDE, WIDE), 1)
    top = jnp.where((row > column) & (col == 0), 0.0, top)
    return (top, basis)


def solution(mesh):
    finer = Mesh(
        mesh.devices.reshape(4, 8, 2, mesh.shape["col"]), ("x", "y", "core", "col")
    )
    return jax.shard_map(
        steps,
        mesh=finer,
        in_specs=(P(ROW, "col"),),
        out_specs=(P(None, "col"), P(ROW, None)),
        check_vma=False,
    )
```

profile of v0, /device:TPU:1, one launch (start us, length us, event | category | flops | bytes accessed | tf_op | source)
XLA Modules:
  0.0 129.5 jit_solution(4068626466648038937)
XLA Ops:
  0.6 11.5 %collective-permute-start.1 = (f32[256,512]{1,0:T(8,128)}, f32[256,512]{1,0:T(8,128)S(1)}, u32[]{:S(2)}, u32[]{:S(2)}) collective-permute-start(f32[256,512]{1,0:T(8,128)} %panels_ref.1), channel_id=1, source_target_pairs={{0,5},{8,13},{16,21},{24,29},{32,37},{40,45},{48,53},{56,61},{64,6... | collective-permute-start | bytes 1572872 | tf_op jit(solution)/shard_map/ppermute | solution.py:197
  12.1 1.3 %collective-permute-start = (f32[256,512]{1,0:T(8,128)}, f32[256,512]{1,0:T(8,128)S(1)}, u32[]{:S(2)}, u32[]{:S(2)}) collective-permute-start(f32[256,512]{1,0:T(8,128)} %panels_ref.1), channel_id=1, source_target_pairs={{0,3},{8,11},{16,19},{24,27},{32,35},{40,43},{48,51},{56,59},{64,6... | collective-permute-start | bytes 1572872 | tf_op jit(solution)/shard_map/ppermute | solution.py:196
  13.5 0.0 copy-start
  13.5 1.0 copy-done
  14.5 1.7 %shard_map.30 = (f32[32,4,640]{2,1,0:T(4,128)S(1)}, f32[32,4,640]{2,1,0:T(4,128)S(1)}) custom-call(s32[1]{0:T(128)} %bitcast.core_ref, f32[256,512]{1,0:T(8,128)S(1)} %copy-done), custom_call_target="tpu_custom_call" | custom-call | flops 600000000 | bytes 2097152 | tf_op jit(solution)/shard_map/pallas_call | solution.py:167
  16.2 2.9 %collective-permute-start.5 = (f32[32,4,640]{2,1,0:T(4,128)S(1)}, f32[32,4,640]{2,1,0:T(4,128)S(1)}, u32[]{:S(2)}, u32[]{:S(2)}) collective-permute-start(f32[32,4,640]{2,1,0:T(4,128)S(1)} %get-tuple-element.11), channel_id=1, source_target_pairs={{0,8},{8,0},{1,9},{9,1},{2,10},{10,2},{3,11},{11,3},{4,12},{12,4},... | collective-permute-start | bytes 983048 | tf_op jit(solution)/shard_map/ppermute | solution.py:186
  19.1 1.2 collective-permute-done.5
  20.3 0.8 add.36
  21.2 9.8 %all-to-all-start = ((f32[32,4,640]{2,1,0:T(4,128)}), f32[32,4,640]{2,1,0:T(4,128)S(1)}, u32[]{:S(2)}, u32[]{:S(2)}) async-start(f32[32,4,640]{2,1,0:T(4,128)} %add.36), calls=%async_computation | async-start | bytes 655360 | tf_op jit(solution)/shard_map/all_to_all | solution.py:178
  31.0 0.0 collective-permute-done.1
  31.0 0.0 collective-permute-done
  31.0 0.1 add_select_fusion.1
  31.2 1.3 %collective-permute-start.3 = (f32[256,512]{1,0:T(8,128)S(1)}, f32[256,512]{1,0:T(8,128)S(1)}, u32[]{:S(2)}, u32[]{:S(2)}) collective-permute-start(f32[256,512]{1,0:T(8,128)S(1)} %add_select_fusion.1), channel_id=1, source_target_pairs={{0,7},{3,2},{8,15},{11,10},{16,23},{19,18},{24,31},{27,26},{32,39}... | collective-permute-start | bytes 1572872 | tf_op jit(solution)/shard_map/ppermute | solution.py:203
  32.5 1.3 %collective-permute-start.2 = (f32[256,512]{1,0:T(8,128)S(1)}, f32[256,512]{1,0:T(8,128)S(1)}, u32[]{:S(2)}, u32[]{:S(2)}) collective-permute-start(f32[256,512]{1,0:T(8,128)S(1)} %add_select_fusion.1), channel_id=1, source_target_pairs={{0,1},{3,4},{5,6},{8,9},{11,12},{13,14},{16,17},{19,20},{21,22},{2... | collective-permute-start | bytes 1572872 | tf_op jit(solution)/shard_map/ppermute | solution.py:202
  33.8 7.6 %all-to-all-done = f32[32,4,640]{2,1,0:T(4,128)S(1)} async-done(((f32[32,4,640]{2,1,0:T(4,128)}), f32[32,4,640]{2,1,0:T(4,128)S(1)}, u32[]{:S(2)}, u32[]{:S(2)}) %all-to-all-start) | async-done | bytes 327712 | tf_op jit(solution)/shard_map/all_to_all | solution.py:178
  41.5 0.1 reduce_sum.18
  41.5 1.3 collective-permute-start.12
  42.8 1.3 collective-permute-start.11
  44.1 1.3 collective-permute-start.10
  45.4 0.0 collective-permute-done.3
  45.4 1.3 collective-permute-start.9
  46.7 0.0 collective-permute-done.2
  46.7 1.3 collective-permute-start.8
  48.0 0.2 add_select_fusion
  48.2 1.0 fusion.11
  49.2 0.0 collective-permute-done.12
  49.2 1.3 collective-permute-start.7
  50.5 1.3 collective-permute-start.6
  51.8 0.1 slice_select_fusion
  51.9 5.7 %collective-permute-start.4 = (f32[256,512]{1,0:T(8,128)S(1)}, f32[256,512]{1,0:T(8,128)S(1)}, u32[]{:S(2)}, u32[]{:S(2)}) collective-permute-start(f32[256,512]{1,0:T(8,128)S(1)} %slice_select_fusion), channel_id=1, source_target_pairs={{0,8},{8,0},{1,9},{9,1},{2,10},{10,2},{3,11},{11,3},{4,12},{12,4},... | collective-permute-start | bytes 1572872 | tf_op jit(solution)/shard_map/ppermute | solution.py:186
  57.7 0.0 collective-permute-done.8
  57.7 0.8 broadcast_in_dim.8
  58.5 6.5 %all-to-all-start.1 = ((f32[32,4,640]{2,1,0:T(4,128)}), f32[32,4,640]{2,1,0:T(4,128)S(1)}, u32[]{:S(2)}, u32[]{:S(2)}) async-start(f32[32,4,640]{2,1,0:T(4,128)} %broadcast_in_dim.8), calls=%async_computation.1 | async-start | bytes 655360 | tf_op jit(solution)/shard_map/all_to_all | solution.py:178
  65.0 0.9 select_add_fusion
  65.9 10.0 %all-to-all-done.1.own_ref = f32[32,4,640]{2,1,0:T(4,128)S(1)} async-done(((f32[32,4,640]{2,1,0:T(4,128)}), f32[32,4,640]{2,1,0:T(4,128)S(1)}, u32[]{:S(2)}, u32[]{:S(2)}) %all-to-all-start.1) | async-done | bytes 327712 | tf_op jit(solution)/shard_map/all_to_all | solution.py:178
  75.9 7.2 %all-to-all-start.2 = ((f32[32,8,512]{2,1,0:T(8,128)}), f32[32,8,512]{2,1,0:T(8,128)S(1)}, u32[]{:S(2)}, u32[]{:S(2)}) async-start(f32[32,8,512]{2,1,0:T(8,128)} %bitcast.1), calls=%async_computation.2 | async-start | bytes 1048576 | tf_op jit(solution)/shard_map/all_to_all | solution.py:178
  83.1 2.9 %collective-permute-start.13 = (f32[32,4,640]{2,1,0:T(4,128)S(1)}, f32[32,4,640]{2,1,0:T(4,128)S(1)}, u32[]{:S(2)}, u32[]{:S(2)}) collective-permute-start(f32[32,4,640]{2,1,0:T(4,128)S(1)} %all-to-all-done.1.own_ref), channel_id=1, source_target_pairs={{0,8},{8,0},{1,9},{9,1},{2,10},{10,2},{3,11},{11,3},{4,12},{12,4},... | collective-permute-start | bytes 983048 | tf_op jit(solution)/shard_map/ppermute | solution.py:186
  86.1 1.2 collective-permute-done.13.other_ref
  87.3 4.9 %shard_map.31.state_ref = f32[512,512]{1,0:T(8,128)S(1)} custom-call(s32[1]{0:T(128)} %bitcast.core_ref, f32[32,4,640]{2,1,0:T(4,128)S(1)} %all-to-all-done.1.own_ref, f32[32,4,640]{2,1,0:T(4,128)S(1)} %collective-permute-done.13.other_ref), custom_call_target="tpu_custom_call" | custom-call | flops 1000000000 | bytes 2097152 | tf_op jit(solution)/shard_map/pallas_call | solution.py:167
  92.3 5.5 %all-to-all-done.2 = f32[32,8,512]{2,1,0:T(8,128)S(1)} async-done(((f32[32,8,512]{2,1,0:T(8,128)}), f32[32,8,512]{2,1,0:T(8,128)S(1)}, u32[]{:S(2)}, u32[]{:S(2)}) %all-to-all-start.2) | async-done | bytes 524320 | tf_op jit(solution)/shard_map/all_to_all | solution.py:178
  97.9 0.9 broadcast_in_dim.18
  98.7 7.3 %all-to-all-start.3 = ((f32[32,8,512]{2,1,0:T(8,128)}), f32[32,8,512]{2,1,0:T(8,128)S(1)}, u32[]{:S(2)}, u32[]{:S(2)}) async-start(f32[32,8,512]{2,1,0:T(8,128)} %broadcast_in_dim.18), calls=%async_computation.3 | async-start | bytes 1048576 | tf_op jit(solution)/shard_map/all_to_all | solution.py:178
  106.0 12.6 %shard_map.32 = f32[512,512]{1,0:T(8,128)S(1)} custom-call(f32[512,512]{1,0:T(8,128)S(1)} %shard_map.31.state_ref), custom_call_target="tpu_custom_call" | custom-call | flops 1000000000 | bytes 2097152 | tf_op jit(solution)/shard_map/pallas_call | solution.py:167
  118.6 1.9 %convolution_multiply_fusion = f32[256,512]{1,0:T(8,128)} fusion(f32[256,512]{1,0:T(8,128)S(1)} %add_select_fusion, f32[512,512]{1,0:T(8,128)S(1)} %shard_map.32), kind=kOutput, calls=%fused_computation.2 | convolution fusion | flops 805437440 | bytes 2097152 | tf_op jit(solution)/shard_map/dot_general | solution.py:32
  120.5 5.5 %collective-permute-start.14 = (f32[256,512]{1,0:T(8,128)S(1)}, f32[256,512]{1,0:T(8,128)S(1)}, u32[]{:S(2)}, u32[]{:S(2)}) collective-permute-start(f32[256,512]{1,0:T(8,128)S(1)} %bitcast.9), channel_id=1, source_target_pairs={{0,8},{8,0},{1,9},{9,1},{2,10},{10,2},{3,11},{11,3},{4,12},{12,4},... | collective-permute-start | bytes 1572872 | tf_op jit(solution)/shard_map/ppermute | solution.py:186
  125.9 1.0 fusion.3
  127.0 0.5 collective-permute-done.14
  127.4 2.0 %fusion = f32[512,512]{1,0:T(8,128)} fusion(f32[512,512]{1,0:T(8,128)S(1)} %fusion.3, f32[256,512]{1,0:T(8,128)S(1)} %collective-permute-done.14, pred[]{:T(512)S(6)} %eq.8, f32[512,512]{1,0:T(8,128)S(1)} %shard_map.32, pred[]{:T(512)S(6)} %eq.9), kind=kOutput, calls=%fused_computation.1 | convolution fusion | flops 806486016 | bytes 3670018 | tf_op jit(solution)/shard_map/dot_general | solution.py:32
  (11 shorter events, 0.1 us)
Async XLA Ops:
  0.6 30.3 %collective-permute-start.1 = (f32[256,512]{1,0:T(8,128)}, f32[256,512]{1,0:T(8,128)S(1)}, u32[]{:S(2)}, u32[]{:S(2)}) collective-permute-start(f32[256,512]{1,0:T(8,128)} %panels_ref.1), channel_id=1, source_target_pairs={{0,5},{8,13},{16,21},{24,29},{32,37},{40,45},{48,53},{56,61},{64,6... | collective-permute-start | bytes 1572872 | tf_op jit(solution)/shard_map/ppermute | solution.py:197
  12.1 18.9 %collective-permute-start = (f32[256,512]{1,0:T(8,128)}, f32[256,512]{1,0:T(8,128)S(1)}, u32[]{:S(2)}, u32[]{:S(2)}) collective-permute-start(f32[256,512]{1,0:T(8,128)} %panels_ref.1), channel_id=1, source_target_pairs={{0,3},{8,11},{16,19},{24,27},{32,35},{40,43},{48,51},{56,59},{64,6... | collective-permute-start | bytes 1572872 | tf_op jit(solution)/shard_map/ppermute | solution.py:196
  13.5 1.1 copy-start
  16.2 4.1 %collective-permute-start.5 = (f32[32,4,640]{2,1,0:T(4,128)S(1)}, f32[32,4,640]{2,1,0:T(4,128)S(1)}, u32[]{:S(2)}, u32[]{:S(2)}) collective-permute-start(f32[32,4,640]{2,1,0:T(4,128)S(1)} %get-tuple-element.11), channel_id=1, source_target_pairs={{0,8},{8,0},{1,9},{9,1},{2,10},{10,2},{3,11},{11,3},{4,12},{12,4},... | collective-permute-start | bytes 983048 | tf_op jit(solution)/shard_map/ppermute | solution.py:186
  21.2 9.8 %copy-start.1 = (f32[256,512]{1,0:T(8,128)S(1)}, f32[256,512]{1,0:T(8,128)}, u32[]{:S(2)}) copy-start(f32[256,512]{1,0:T(8,128)} %panels_ref.1) | copy-start | bytes 1572868
  21.2 20.3 %all-to-all-start = ((f32[32,4,640]{2,1,0:T(4,128)}), f32[32,4,640]{2,1,0:T(4,128)S(1)}, u32[]{:S(2)}, u32[]{:S(2)}) async-start(f32[32,4,640]{2,1,0:T(4,128)} %add.36), calls=%async_computation | async-start | bytes 655360 | tf_op jit(solution)/shard_map/all_to_all | solution.py:178
  31.2 14.3 %collective-permute-start.3 = (f32[256,512]{1,0:T(8,128)S(1)}, f32[256,512]{1,0:T(8,128)S(1)}, u32[]{:S(2)}, u32[]{:S(2)}) collective-permute-start(f32[256,512]{1,0:T(8,128)S(1)} %add_select_fusion.1), channel_id=1, source_target_pairs={{0,7},{3,2},{8,15},{11,10},{16,23},{19,18},{24,31},{27,26},{32,39}... | collective-permute-start | bytes 1572872 | tf_op jit(solution)/shard_map/ppermute | solution.py:203
  32.5 14.2 %collective-permute-start.2 = (f32[256,512]{1,0:T(8,128)S(1)}, f32[256,512]{1,0:T(8,128)S(1)}, u32[]{:S(2)}, u32[]{:S(2)}) collective-permute-start(f32[256,512]{1,0:T(8,128)S(1)} %add_select_fusion.1), channel_id=1, source_target_pairs={{0,1},{3,4},{5,6},{8,9},{11,12},{13,14},{16,17},{19,20},{21,22},{2... | collective-permute-start | bytes 1572872 | tf_op jit(solution)/shard_map/ppermute | solution.py:202
  41.5 7.7 %collective-permute-start.12 = (f32[4,640]{1,0:T(4,128)S(1)}, f32[4,640]{1,0:T(4,128)S(1)}, u32[]{:S(2)}, u32[]{:S(2)}) collective-permute-start(f32[4,640]{1,0:T(4,128)S(1)} %reduce_sum.18), channel_id=1, source_target_pairs={{0,7},{8,15},{16,23},{24,31},{32,39},{40,47},{48,55},{56,63},{64,7... | collective-permute-start | bytes 30728 | tf_op jit(solution)/shard_map/ppermute | solution.py:206
  42.8 7.7 %collective-permute-start.11 = (f32[4,640]{1,0:T(4,128)S(1)}, f32[4,640]{1,0:T(4,128)S(1)}, u32[]{:S(2)}, u32[]{:S(2)}) collective-permute-start(f32[4,640]{1,0:T(4,128)S(1)} %reduce_sum.18), channel_id=1, source_target_pairs={{0,6},{8,14},{16,22},{24,30},{32,38},{40,46},{48,54},{56,62},{64,7... | collective-permute-start | bytes 30728 | tf_op jit(solution)/shard_map/ppermute | solution.py:206
  44.1 7.8 %collective-permute-start.10 = (f32[4,640]{1,0:T(4,128)S(1)}, f32[4,640]{1,0:T(4,128)S(1)}, u32[]{:S(2)}, u32[]{:S(2)}) collective-permute-start(f32[4,640]{1,0:T(4,128)S(1)} %reduce_sum.18), channel_id=1, source_target_pairs={{0,5},{8,13},{16,21},{24,29},{32,37},{40,45},{48,53},{56,61},{64,6... | collective-permute-start | bytes 30728 | tf_op jit(solution)/shard_map/ppermute | solution.py:206
  45.4 12.2 %collective-permute-start.9 = (f32[4,640]{1,0:T(4,128)S(1)}, f32[4,640]{1,0:T(4,128)S(1)}, u32[]{:S(2)}, u32[]{:S(2)}) collective-permute-start(f32[4,640]{1,0:T(4,128)S(1)} %reduce_sum.18), channel_id=1, source_target_pairs={{0,4},{8,12},{16,20},{24,28},{32,36},{40,44},{48,52},{56,60},{64,6... | collective-permute-start | bytes 30728 | tf_op jit(solution)/shard_map/ppermute | solution.py:206
  46.7 10.9 %collective-permute-start.8 = (f32[4,640]{1,0:T(4,128)S(1)}, f32[4,640]{1,0:T(4,128)S(1)}, u32[]{:S(2)}, u32[]{:S(2)}) collective-permute-start(f32[4,640]{1,0:T(4,128)S(1)} %reduce_sum.18), channel_id=1, source_target_pairs={{0,3},{8,11},{16,19},{24,27},{32,35},{40,43},{48,51},{56,59},{64,6... | collective-permute-start | bytes 30728 | tf_op jit(solution)/shard_map/ppermute | solution.py:206
  49.2 8.4 %collective-permute-start.7 = (f32[4,640]{1,0:T(4,128)S(1)}, f32[4,640]{1,0:T(4,128)S(1)}, u32[]{:S(2)}, u32[]{:S(2)}) collective-permute-start(f32[4,640]{1,0:T(4,128)S(1)} %reduce_sum.18), channel_id=1, source_target_pairs={{0,2},{8,10},{16,18},{24,26},{32,34},{40,42},{48,50},{56,58},{64,6... | collective-permute-start | bytes 30728 | tf_op jit(solution)/shard_map/ppermute | solution.py:206
  50.5 7.1 %collective-permute-start.6 = (f32[4,640]{1,0:T(4,128)S(1)}, f32[4,640]{1,0:T(4,128)S(1)}, u32[]{:S(2)}, u32[]{:S(2)}) collective-permute-start(f32[4,640]{1,0:T(4,128)S(1)} %reduce_sum.18), channel_id=1, source_target_pairs={{0,1},{8,9},{16,17},{24,25},{32,33},{40,41},{48,49},{56,57},{64,65... | collective-permute-start | bytes 30728 | tf_op jit(solution)/shard_map/ppermute | solution.py:206
  51.9 13.0 %collective-permute-start.4 = (f32[256,512]{1,0:T(8,128)S(1)}, f32[256,512]{1,0:T(8,128)S(1)}, u32[]{:S(2)}, u32[]{:S(2)}) collective-permute-start(f32[256,512]{1,0:T(8,128)S(1)} %slice_select_fusion), channel_id=1, source_target_pairs={{0,8},{8,0},{1,9},{9,1},{2,10},{10,2},{3,11},{11,3},{4,12},{12,4},... | collective-permute-start | bytes 1572872 | tf_op jit(solution)/shard_map/ppermute | solution.py:186
  58.5 17.4 %all-to-all-start.1 = ((f32[32,4,640]{2,1,0:T(4,128)}), f32[32,4,640]{2,1,0:T(4,128)S(1)}, u32[]{:S(2)}, u32[]{:S(2)}) async-start(f32[32,4,640]{2,1,0:T(4,128)} %broadcast_in_dim.8), calls=%async_computation.1 | async-start | bytes 655360 | tf_op jit(solution)/shard_map/all_to_all | solution.py:178
  75.9 21.9 %all-to-all-start.2 = ((f32[32,8,512]{2,1,0:T(8,128)}), f32[32,8,512]{2,1,0:T(8,128)S(1)}, u32[]{:S(2)}, u32[]{:S(2)}) async-start(f32[32,8,512]{2,1,0:T(8,128)} %bitcast.1), calls=%async_computation.2 | async-start | bytes 1048576 | tf_op jit(solution)/shard_map/all_to_all | solution.py:178
  83.1 4.2 %collective-permute-start.13 = (f32[32,4,640]{2,1,0:T(4,128)S(1)}, f32[32,4,640]{2,1,0:T(4,128)S(1)}, u32[]{:S(2)}, u32[]{:S(2)}) collective-permute-start(f32[32,4,640]{2,1,0:T(4,128)S(1)} %all-to-all-done.1.own_ref), channel_id=1, source_target_pairs={{0,8},{8,0},{1,9},{9,1},{2,10},{10,2},{3,11},{11,3},{4,12},{12,4},... | collective-permute-start | bytes 983048 | tf_op jit(solution)/shard_map/ppermute | solution.py:186
  98.7 21.8 %all-to-all-start.3 = ((f32[32,8,512]{2,1,0:T(8,128)}), f32[32,8,512]{2,1,0:T(8,128)S(1)}, u32[]{:S(2)}, u32[]{:S(2)}) async-start(f32[32,8,512]{2,1,0:T(8,128)} %broadcast_in_dim.18), calls=%async_computation.3 | async-start | bytes 1048576 | tf_op jit(solution)/shard_map/all_to_all | solution.py:178
  120.5 7.0 %collective-permute-start.14 = (f32[256,512]{1,0:T(8,128)S(1)}, f32[256,512]{1,0:T(8,128)S(1)}, u32[]{:S(2)}, u32[]{:S(2)}) collective-permute-start(f32[256,512]{1,0:T(8,128)S(1)} %bitcast.9), channel_id=1, source_target_pairs={{0,8},{8,0},{1,9},{9,1},{2,10},{10,2},{3,11},{11,3},{4,12},{12,4},... | collective-permute-start | bytes 1572872 | tf_op jit(solution)/shard_map/ppermute | solution.py:186
where the time goes:
time: 130 us; the launch traced here: 129 us
  starting transfers between devices  72.2 us (56%)
  waiting for transfers between devices  26.2 us (20%)
  Pallas kernels  19.2 us (15%)
  matrix products  5.94 us (5%)
  local copies, waits for them, and re-layouts  2.68 us (2%)
  other arithmetic  2.26 us (2%)
    all_to_all x4, starting transfers between devices, exchange(): return lax.all_to_all(blocks, axis, 0, 0, tiled=True)  30.8 us
    all_to_all x4, waiting for transfers between devices, exchange(): return lax.all_to_all(blocks, axis, 0, 0, tiled=True)  23.2 us
    pallas_call x3, Pallas kernels, call(): pl.pallas_call(kernel, out_shape=[jax.ShapeDtypeStruct(shape, jnp.float32...  19.2 us
    ppermute x4, starting transfers between devices, swapped(): return lax.ppermute(array, 'core', [(0, 1), (1, 0)])  16.9 us
    ppermute x1, starting transfers between devices, steps(): down = lax.ppermute(matrix, 'col', [(0, 5)])  11.5 us
    ppermute x7, starting transfers between devices, steps(): lax.ppermute(gram_part, 'col', [(0, k)])  9.02 us
    dot_general x3, matrix products, product(): jnp.dot(left, right, precision=HIGHEST, preferred_element_type=jnp.float32)  4.91 us
    ppermute x4, waiting for transfers between devices, swapped(): return lax.ppermute(array, 'core', [(0, 1), (1, 0)])  2.95 us
  transfers between devices with their start and end apart: 19, of which 6 were waited for; matrix products, arithmetic and copies ran while one was open for 5% of the time, Pallas kernels for 15%

commit v1 on v0

--- a/solution.py
+++ b/solution.py
@@ -186,6 +186,22 @@
     return lax.ppermute(array, "core", [(0, 1), (1, 0)])
 
 
+def gathered_along_x(array):
+    count = lax.axis_size("x")
+    pieces = [array]
+    for step in range(1, count):
+        pairs = [(i, (i + step) % count) for i in range(count)]
+        pieces.append(lax.ppermute(array, "x", pairs))
+    lines = []
+    for place in range(count):
+        line = pieces[0]
+        for step in range(1, count):
+            source = lax.rem(lax.axis_index("x") + count - step, count)
+            line = jnp.where(source == place, pieces[step], line)
+        lines.append(line)
+    return jnp.concatenate(lines)
+
+
 def steps(matrix):
     rows_all = matrix.shape[0] * lax.axis_size(ROW)
     chips = lax.axis_size(PLANE)
@@ -201,12 +217,8 @@
     panels = jnp.where(col == 0, matrix, up + down)
     up = lax.ppermute(panels, "col", [(0, 1), (3, 4), (5, 6)])
     down = lax.ppermute(panels, "col", [(0, 7), (3, 2)])
-    gram_part = gram_part.sum(axis=0)
-    copies = [
-        lax.ppermute(gram_part, "col", [(0, k)]) for k in range(1, lax.axis_size("col"))
-    ]
-    gram_part = jnp.where(col == 0, gram_part, sum(copies))
-    own = exchange(spread(gram_part, chips), PLANE)
+    gram_part = exchange(spread(gram_part.sum(axis=0), lax.axis_size("col")), "col")
+    own = exchange(spread(gram_part[0], lax.axis_size("y")), "y")
     panels = jnp.where((col == 0) | (col == 3) | (col == 5), panels, up + down)
     panels = lax.optimization_barrier(panels)
     products = inner(panels, matrix).reshape(2, -1, WIDE)
@@ -214,6 +226,7 @@
     half = mine + swapped(jnp.where(core == 0, products[1], products[0]))
     half, own = lax.optimization_barrier((half, own))
     part = exchange(half.reshape(chips, -1, WIDE), PLANE)
+    own = gathered_along_x(own)
     (state,) = call(start_kernel, (which, own, swapped(own)), [(WIDE, WIDE)], 1_000_000_000)
     part, state = lax.optimization_barrier((part, state))
     half = exchange(spread(part.sum(axis=0), chips), PLANE).reshape(-1, WIDE)

time: 130 us -> 147 us (1.13)
  blocking collectives: 0 us -> 11.3 us
  waiting for transfers between devices: 26.2 us -> 28.8 us
  other arithmetic: 2.26 us -> 4.45 us
    all_to_all x0 -> x1, blocking collectives: none -> 11.3 us  [exchange(): return lax.all_to_all(blocks, axis, 0, 0, tiled=True)]
    all_to_all x4, waiting for transfers between devices: 23.2 us -> 12 us  [exchange(): return lax.all_to_all(blocks, axis, 0, 0, tiled=True)]
    ppermute x1, waiting for transfers between devices: 0.01 us -> 9.53 us  [steps(): down = lax.ppermute(matrix, 'col', [(0, 5)])]
    ppermute x7 -> x3, waiting for transfers between devices: 0.02 us -> 3.02 us  [gathered_along_x(): pieces.append(lax.ppermute(array, 'x', pairs))]
    all_to_all x4, starting transfers between devices: 30.8 us -> 28.1 us  [exchange(): return lax.all_to_all(blocks, axis, 0, 0, tiled=True)]
    ppermute x4, starting transfers between devices: 16.9 us -> 18.6 us  [swapped(): return lax.ppermute(array, 'core', [(0, 1), (1, 0)])]
    ppermute x7 -> x3, starting transfers between devices: 9.02 us -> 10.5 us  [gathered_along_x(): pieces.append(lax.ppermute(array, 'x', pairs))]
  transfers between devices with their start and end apart: 19 -> 15, of which waited for: 6 -> 9; matrix products, arithmetic and copies ran while one was open for 5% -> 5% of each run, Pallas kernels for 15% -> 13%
where the time goes in v1:
time: 147 us; the launch traced here: 146 us
  starting transfers between devices  73.4 us (50%)
  waiting for transfers between devices  28.8 us (20%)
  Pallas kernels  19.2 us (13%)
  blocking collectives  11.3 us (8%)
  matrix products  5.94 us (4%)
  other arithmetic  4.45 us (3%)
  local copies, waits for them, and re-layouts  1.52 us (1%)
    all_to_all x4, starting transfers between devices, exchange(): return lax.all_to_all(blocks, axis, 0, 0, tiled=True)  28.1 us
    pallas_call x3, Pallas kernels, call(): pl.pallas_call(kernel, out_shape=[jax.ShapeDtypeStruct(shape, jnp.float32...  19.2 us
    ppermute x4, starting transfers between devices, swapped(): return lax.ppermute(array, 'core', [(0, 1), (1, 0)])  18.6 us
    all_to_all x4, waiting for transfers between devices, exchange(): return lax.all_to_all(blocks, axis, 0, 0, tiled=True)  12 us
    ppermute x1, starting transfers between devices, steps(): down = lax.ppermute(matrix, 'col', [(0, 5)])  11.5 us
    all_to_all x1, blocking collectives, exchange(): return lax.all_to_all(blocks, axis, 0, 0, tiled=True)  11.3 us
    ppermute x3, starting transfers between devices, gathered_along_x(): pieces.append(lax.ppermute(array, 'x', pairs))  10.5 us
    ppermute x1, waiting for transfers between devices, steps(): down = lax.ppermute(matrix, 'col', [(0, 5)])  9.53 us
  transfers between devices with their start and end apart: 15, of which 9 were waited for; matrix products, arithmetic and copies ran while one was open for 5% of the time, Pallas kernels for 13%

profile of v1, /device:TPU:1, one launch (start us, length us, event | category | flops | bytes accessed | tf_op | source)
XLA Modules:
  0.0 145.6 jit_solution(12105567296393454242)
XLA Ops:
  0.6 11.5 %collective-permute-start.1 = (f32[256,512]{1,0:T(8,128)}, f32[256,512]{1,0:T(8,128)S(1)}, u32[]{:S(2)}, u32[]{:S(2)}) collective-permute-start(f32[256,512]{1,0:T(8,128)} %panels_ref.1), channel_id=1, source_target_pairs={{0,5},{8,13},{16,21},{24,29},{32,37},{40,45},{48,53},{56,61},{64,6... | collective-permute-start | bytes 1572872 | tf_op jit(solution)/shard_map/ppermute | solution.py:213
  12.1 1.3 collective-permute-start
  13.5 0.0 copy-start
  13.5 9.5 %collective-permute-done.1 = f32[256,512]{1,0:T(8,128)S(1)} collective-permute-done((f32[256,512]{1,0:T(8,128)}, f32[256,512]{1,0:T(8,128)S(1)}, u32[]{:S(2)}, u32[]{:S(2)}) %collective-permute-start.1) | collective-permute-done | bytes 524320 | tf_op jit(solution)/shard_map/ppermute | solution.py:213
  23.0 1.3 collective-permute-done
  24.3 1.2 add_select_fusion.1
  25.5 1.3 collective-permute-start.3
  26.9 2.1 %collective-permute-start.2 = (f32[256,512]{1,0:T(8,128)S(1)}, f32[256,512]{1,0:T(8,128)}, u32[]{:S(2)}, u32[]{:S(2)}) collective-permute-start(f32[256,512]{1,0:T(8,128)S(1)} %add_select_fusion.1), channel_id=1, source_target_pairs={{0,1},{3,4},{5,6},{8,9},{11,12},{13,14},{16,17},{19,20},{21,22},{2... | collective-permute-start | bytes 1572872 | tf_op jit(solution)/shard_map/ppermute | solution.py:218
  29.0 1.7 %shard_map.30 = (f32[32,4,640]{2,1,0:T(4,128)S(1)}, f32[32,4,640]{2,1,0:T(4,128)S(1)}) custom-call(s32[1]{0:T(128)} %bitcast.core_ref, f32[256,512]{1,0:T(8,128)S(1)} %copy-done), custom_call_target="tpu_custom_call" | custom-call | flops 600000000 | bytes 2097152 | tf_op jit(solution)/shard_map/pallas_call | solution.py:167
  30.7 3.4 %collective-permute-start.5 = (f32[32,4,640]{2,1,0:T(4,128)S(1)}, f32[32,4,640]{2,1,0:T(4,128)S(1)}, u32[]{:S(2)}, u32[]{:S(2)}) collective-permute-start(f32[32,4,640]{2,1,0:T(4,128)S(1)} %get-tuple-element.11), channel_id=1, source_target_pairs={{0,8},{8,0},{1,9},{9,1},{2,10},{10,2},{3,11},{11,3},{4,12},{12,4},... | collective-permute-start | bytes 983048 | tf_op jit(solution)/shard_map/ppermute | solution.py:186
  34.1 1.2 collective-permute-done.5
  35.3 0.8 add.39
  36.1 9.7 %all-to-all-start = ((f32[32,4,640]{2,1,0:T(4,128)}), f32[32,4,640]{2,1,0:T(4,128)S(1)}, u32[]{:S(2)}, u32[]{:S(2)}) async-start(f32[32,4,640]{2,1,0:T(4,128)} %add.39), calls=%async_computation | async-start | bytes 655360 | tf_op jit(solution)/shard_map/all_to_all | solution.py:178
  45.8 0.0 collective-permute-done.3
  45.8 0.0 collective-permute-done.2
  45.9 1.2 add_select_fusion
  47.1 1.0 fusion.11
  48.1 0.1 slice_select_fusion
  48.2 2.6 %collective-permute-start.4 = (f32[256,512]{1,0:T(8,128)S(1)}, f32[256,512]{1,0:T(8,128)S(1)}, u32[]{:S(2)}, u32[]{:S(2)}) collective-permute-start(f32[256,512]{1,0:T(8,128)S(1)} %slice_select_fusion), channel_id=1, source_target_pairs={{0,8},{8,0},{1,9},{9,1},{2,10},{10,2},{3,11},{11,3},{4,12},{12,4},... | collective-permute-start | bytes 1572872 | tf_op jit(solution)/shard_map/ppermute | solution.py:186
  50.8 5.6 %all-to-all-done = f32[32,4,640]{2,1,0:T(4,128)S(1)} async-done(((f32[32,4,640]{2,1,0:T(4,128)}), f32[32,4,640]{2,1,0:T(4,128)S(1)}, u32[]{:S(2)}, u32[]{:S(2)}) %all-to-all-start) | async-done | bytes 327712 | tf_op jit(solution)/shard_map/all_to_all | solution.py:178
  56.3 0.1 reduce_sum.18
  56.4 11.3 %all_to_all.25 = f32[8,4,640]{2,1,0:T(4,128)S(1)} all-to-all(f32[8,4,640]{2,1,0:T(4,128)S(1)} %broadcast_in_dim.24), channel_id=1, replica_groups=mesh['x'=4,'y'=8,'core'=2,'col'=8] {'col'}, dimensions={0} | all-to-all | bytes 163840 | tf_op jit(solution)/shard_map/all_to_all | solution.py:178
  67.7 0.6 broadcast_in_dim.26
  68.4 5.5 %all-to-all-start.2 = ((f32[8,4,640]{2,1,0:T(4,128)}), f32[8,4,640]{2,1,0:T(4,128)S(1)}, u32[]{:S(2)}, u32[]{:S(2)}) async-start(f32[8,4,640]{2,1,0:T(4,128)} %broadcast_in_dim.26), calls=%async_computation.2 | async-start | bytes 163840 | tf_op jit(solution)/shard_map/all_to_all | solution.py:178
  73.9 0.0 collective-permute-done.4
  73.9 0.9 select_add_fusion
  74.8 6.5 %all-to-all-done.2 = f32[8,4,640]{2,1,0:T(4,128)S(1)} async-done(((f32[8,4,640]{2,1,0:T(4,128)}), f32[8,4,640]{2,1,0:T(4,128)S(1)}, u32[]{:S(2)}, u32[]{:S(2)}) %all-to-all-start.2) | async-done | bytes 81952 | tf_op jit(solution)/shard_map/all_to_all | solution.py:178
  81.3 3.9 %all-to-all-start.3 = ((f32[32,8,512]{2,1,0:T(8,128)}), f32[32,8,512]{2,1,0:T(8,128)S(1)}, u32[]{:S(2)}, u32[]{:S(2)}) async-start(f32[32,8,512]{2,1,0:T(8,128)} %bitcast.2), calls=%async_computation.3 | async-start | bytes 1048576 | tf_op jit(solution)/shard_map/all_to_all | solution.py:178
  85.2 3.1 %collective-permute-start.8 = (f32[8,4,640]{2,1,0:T(4,128)S(1)}, f32[8,4,640]{2,1,0:T(4,128)S(1)}, u32[]{:S(2)}, u32[]{:S(2)}) collective-permute-start(f32[8,4,640]{2,1,0:T(4,128)S(1)} %all-to-all-done.2), channel_id=1, source_target_pairs={{0,128},{128,256},{256,384},{384,0},{1,129},{129,257},{257,385},{3... | collective-permute-start | bytes 245768 | tf_op jit(solution)/shard_map/ppermute | solution.py:194
  88.2 4.4 %collective-permute-start.7 = (f32[8,4,640]{2,1,0:T(4,128)S(1)}, f32[8,4,640]{2,1,0:T(4,128)S(1)}, u32[]{:S(2)}, u32[]{:S(2)}) collective-permute-start(f32[8,4,640]{2,1,0:T(4,128)S(1)} %all-to-all-done.2), channel_id=1, source_target_pairs={{0,256},{128,384},{256,0},{384,128},{1,257},{129,385},{257,1},{385... | collective-permute-start | bytes 245768 | tf_op jit(solution)/shard_map/ppermute | solution.py:194
  92.7 3.0 %collective-permute-start.6 = (f32[8,4,640]{2,1,0:T(4,128)S(1)}, f32[8,4,640]{2,1,0:T(4,128)S(1)}, u32[]{:S(2)}, u32[]{:S(2)}) collective-permute-start(f32[8,4,640]{2,1,0:T(4,128)S(1)} %all-to-all-done.2), channel_id=1, source_target_pairs={{0,384},{128,0},{256,128},{384,256},{1,385},{129,1},{257,129},{385... | collective-permute-start | bytes 245768 | tf_op jit(solution)/shard_map/ppermute | solution.py:194
  95.7 0.0 collective-permute-done.8
  95.7 1.4 collective-permute-done.7
  97.1 1.7 %collective-permute-done.6 = f32[8,4,640]{2,1,0:T(4,128)S(1)} collective-permute-done((f32[8,4,640]{2,1,0:T(4,128)S(1)}, f32[8,4,640]{2,1,0:T(4,128)S(1)}, u32[]{:S(2)}, u32[]{:S(2)}) %collective-permute-start.6) | collective-permute-done | bytes 81952 | tf_op jit(solution)/shard_map/ppermute | solution.py:194
  98.8 0.1 pad_maximum_fusion.own_ref
  98.9 7.6 %collective-permute-start.9 = (f32[32,4,640]{2,1,0:T(4,128)S(1)}, f32[32,4,640]{2,1,0:T(4,128)S(1)}, u32[]{:S(2)}, u32[]{:S(2)}) collective-permute-start(f32[32,4,640]{2,1,0:T(4,128)S(1)} %pad_maximum_fusion.own_ref), channel_id=1, source_target_pairs={{0,8},{8,0},{1,9},{9,1},{2,10},{10,2},{3,11},{11,3},{4,12},{12,4},... | collective-permute-start | bytes 983048 | tf_op jit(solution)/shard_map/ppermute | solution.py:186
  106.5 1.2 collective-permute-done.9.other_ref
  107.8 4.9 %shard_map.31.state_ref = f32[512,512]{1,0:T(8,128)S(1)} custom-call(s32[1]{0:T(128)} %bitcast.core_ref, f32[32,4,640]{2,1,0:T(4,128)S(1)} %pad_maximum_fusion.own_ref, f32[32,4,640]{2,1,0:T(4,128)S(1)} %collective-permute-done.9.other_ref), custom_call_target="tpu_custom_call" | custom-call | flops 1000000000 | bytes 2097152 | tf_op jit(solution)/shard_map/pallas_call | solution.py:167
  112.7 0.0 all-to-all-done.3
  112.8 0.9 broadcast_in_dim.27
  113.6 9.0 %all-to-all-start.4 = ((f32[32,8,512]{2,1,0:T(8,128)}), f32[32,8,512]{2,1,0:T(8,128)S(1)}, u32[]{:S(2)}, u32[]{:S(2)}) async-start(f32[32,8,512]{2,1,0:T(8,128)} %broadcast_in_dim.27), calls=%async_computation.4 | async-start | bytes 1048576 | tf_op jit(solution)/shard_map/all_to_all | solution.py:178
  122.7 12.6 %shard_map.32 = f32[512,512]{1,0:T(8,128)S(1)} custom-call(f32[512,512]{1,0:T(8,128)S(1)} %shard_map.31.state_ref), custom_call_target="tpu_custom_call" | custom-call | flops 1000000000 | bytes 2097152 | tf_op jit(solution)/shard_map/pallas_call | solution.py:167
  135.2 1.9 %convolution_multiply_fusion = f32[256,512]{1,0:T(8,128)} fusion(f32[256,512]{1,0:T(8,128)S(1)} %add_select_fusion, f32[512,512]{1,0:T(8,128)S(1)} %shard_map.32), kind=kOutput, calls=%fused_computation.2 | convolution fusion | flops 805437440 | bytes 2097152 | tf_op jit(solution)/shard_map/dot_general | solution.py:32
  137.1 0.0 all-to-all-done.4
  137.1 5.0 %collective-permute-start.10 = (f32[256,512]{1,0:T(8,128)S(1)}, f32[256,512]{1,0:T(8,128)S(1)}, u32[]{:S(2)}, u32[]{:S(2)}) collective-permute-start(f32[256,512]{1,0:T(8,128)S(1)} %bitcast.19), channel_id=1, source_target_pairs={{0,8},{8,0},{1,9},{9,1},{2,10},{10,2},{3,11},{11,3},{4,12},{12,4},... | collective-permute-start | bytes 1572872 | tf_op jit(solution)/shard_map/ppermute | solution.py:186
  142.1 1.0 fusion.3
  143.1 0.5 collective-permute-done.10
  143.6 2.0 %fusion = f32[512,512]{1,0:T(8,128)} fusion(f32[512,512]{1,0:T(8,128)S(1)} %fusion.3, f32[256,512]{1,0:T(8,128)S(1)} %collective-permute-done.10, pred[]{:T(512)S(6)} %eq.53, f32[512,512]{1,0:T(8,128)S(1)} %shard_map.32, pred[]{:T(512)S(6)} %eq.54), kind=kOutput, calls=%fused_computation.1 | convolution fusion | flops 806486016 | bytes 3670018 | tf_op jit(solution)/shard_map/dot_general | solution.py:32
  (5 shorter events, 0.1 us)
Async XLA Ops:
  0.6 22.4 %collective-permute-start.1 = (f32[256,512]{1,0:T(8,128)}, f32[256,512]{1,0:T(8,128)S(1)}, u32[]{:S(2)}, u32[]{:S(2)}) collective-permute-start(f32[256,512]{1,0:T(8,128)} %panels_ref.1), channel_id=1, source_target_pairs={{0,5},{8,13},{16,21},{24,29},{32,37},{40,45},{48,53},{56,61},{64,6... | collective-permute-start | bytes 1572872 | tf_op jit(solution)/shard_map/ppermute | solution.py:213
  12.1 12.2 %collective-permute-start = (f32[256,512]{1,0:T(8,128)}, f32[256,512]{1,0:T(8,128)S(1)}, u32[]{:S(2)}, u32[]{:S(2)}) collective-permute-start(f32[256,512]{1,0:T(8,128)} %panels_ref.1), channel_id=1, source_target_pairs={{0,3},{8,11},{16,19},{24,27},{32,35},{40,43},{48,51},{56,59},{64,6... | collective-permute-start | bytes 1572872 | tf_op jit(solution)/shard_map/ppermute | solution.py:212
  13.5 15.5 %copy-start = (f32[256,512]{1,0:T(8,128)S(1)}, f32[256,512]{1,0:T(8,128)}, u32[]{:S(2)}) copy-start(f32[256,512]{1,0:T(8,128)} %panels_ref.1) | copy-start | bytes 1572868
  25.5 20.3 %collective-permute-start.3 = (f32[256,512]{1,0:T(8,128)S(1)}, f32[256,512]{1,0:T(8,128)S(1)}, u32[]{:S(2)}, u32[]{:S(2)}) collective-permute-start(f32[256,512]{1,0:T(8,128)S(1)} %add_select_fusion.1), channel_id=1, source_target_pairs={{0,7},{3,2},{8,15},{11,10},{16,23},{19,18},{24,31},{27,26},{32,39}... | collective-permute-start | bytes 1572872 | tf_op jit(solution)/shard_map/ppermute | solution.py:219
  26.9 19.0 %collective-permute-start.2 = (f32[256,512]{1,0:T(8,128)S(1)}, f32[256,512]{1,0:T(8,128)}, u32[]{:S(2)}, u32[]{:S(2)}) collective-permute-start(f32[256,512]{1,0:T(8,128)S(1)} %add_select_fusion.1), channel_id=1, source_target_pairs={{0,1},{3,4},{5,6},{8,9},{11,12},{13,14},{16,17},{19,20},{21,22},{2... | collective-permute-start | bytes 1572872 | tf_op jit(solution)/shard_map/ppermute | solution.py:218
  30.7 4.7 %collective-permute-start.5 = (f32[32,4,640]{2,1,0:T(4,128)S(1)}, f32[32,4,640]{2,1,0:T(4,128)S(1)}, u32[]{:S(2)}, u32[]{:S(2)}) collective-permute-start(f32[32,4,640]{2,1,0:T(4,128)S(1)} %get-tuple-element.11), channel_id=1, source_target_pairs={{0,8},{8,0},{1,9},{9,1},{2,10},{10,2},{3,11},{11,3},{4,12},{12,4},... | collective-permute-start | bytes 983048 | tf_op jit(solution)/shard_map/ppermute | solution.py:186
  36.1 20.2 %all-to-all-start = ((f32[32,4,640]{2,1,0:T(4,128)}), f32[32,4,640]{2,1,0:T(4,128)S(1)}, u32[]{:S(2)}, u32[]{:S(2)}) async-start(f32[32,4,640]{2,1,0:T(4,128)} %add.39), calls=%async_computation | async-start | bytes 655360 | tf_op jit(solution)/shard_map/all_to_all | solution.py:178
  48.2 25.7 %collective-permute-start.4 = (f32[256,512]{1,0:T(8,128)S(1)}, f32[256,512]{1,0:T(8,128)S(1)}, u32[]{:S(2)}, u32[]{:S(2)}) collective-permute-start(f32[256,512]{1,0:T(8,128)S(1)} %slice_select_fusion), channel_id=1, source_target_pairs={{0,8},{8,0},{1,9},{9,1},{2,10},{10,2},{3,11},{11,3},{4,12},{12,4},... | collective-permute-start | bytes 1572872 | tf_op jit(solution)/shard_map/ppermute | solution.py:186
  68.4 12.9 %all-to-all-start.2 = ((f32[8,4,640]{2,1,0:T(4,128)}), f32[8,4,640]{2,1,0:T(4,128)S(1)}, u32[]{:S(2)}, u32[]{:S(2)}) async-start(f32[8,4,640]{2,1,0:T(4,128)} %broadcast_in_dim.26), calls=%async_computation.2 | async-start | bytes 163840 | tf_op jit(solution)/shard_map/all_to_all | solution.py:178
  81.3 31.5 %all-to-all-start.3 = ((f32[32,8,512]{2,1,0:T(8,128)}), f32[32,8,512]{2,1,0:T(8,128)S(1)}, u32[]{:S(2)}, u32[]{:S(2)}) async-start(f32[32,8,512]{2,1,0:T(8,128)} %bitcast.2), calls=%async_computation.3 | async-start | bytes 1048576 | tf_op jit(solution)/shard_map/all_to_all | solution.py:178
  85.2 10.6 %collective-permute-start.8 = (f32[8,4,640]{2,1,0:T(4,128)S(1)}, f32[8,4,640]{2,1,0:T(4,128)S(1)}, u32[]{:S(2)}, u32[]{:S(2)}) collective-permute-start(f32[8,4,640]{2,1,0:T(4,128)S(1)} %all-to-all-done.2), channel_id=1, source_target_pairs={{0,128},{128,256},{256,384},{384,0},{1,129},{129,257},{257,385},{3... | collective-permute-start | bytes 245768 | tf_op jit(solution)/shard_map/ppermute | solution.py:194
  88.2 8.8 %collective-permute-start.7 = (f32[8,4,640]{2,1,0:T(4,128)S(1)}, f32[8,4,640]{2,1,0:T(4,128)S(1)}, u32[]{:S(2)}, u32[]{:S(2)}) collective-permute-start(f32[8,4,640]{2,1,0:T(4,128)S(1)} %all-to-all-done.2), channel_id=1, source_target_pairs={{0,256},{128,384},{256,0},{384,128},{1,257},{129,385},{257,1},{385... | collective-permute-start | bytes 245768 | tf_op jit(solution)/shard_map/ppermute | solution.py:194
  92.7 6.1 %collective-permute-start.6 = (f32[8,4,640]{2,1,0:T(4,128)S(1)}, f32[8,4,640]{2,1,0:T(4,128)S(1)}, u32[]{:S(2)}, u32[]{:S(2)}) collective-permute-start(f32[8,4,640]{2,1,0:T(4,128)S(1)} %all-to-all-done.2), channel_id=1, source_target_pairs={{0,384},{128,0},{256,128},{384,256},{1,385},{129,1},{257,129},{385... | collective-permute-start | bytes 245768 | tf_op jit(solution)/shard_map/ppermute | solution.py:194
  98.9 8.9 %collective-permute-start.9 = (f32[32,4,640]{2,1,0:T(4,128)S(1)}, f32[32,4,640]{2,1,0:T(4,128)S(1)}, u32[]{:S(2)}, u32[]{:S(2)}) collective-permute-start(f32[32,4,640]{2,1,0:T(4,128)S(1)} %pad_maximum_fusion.own_ref), channel_id=1, source_target_pairs={{0,8},{8,0},{1,9},{9,1},{2,10},{10,2},{3,11},{11,3},{4,12},{12,4},... | collective-permute-start | bytes 983048 | tf_op jit(solution)/shard_map/ppermute | solution.py:186
  113.6 23.4 %all-to-all-start.4 = ((f32[32,8,512]{2,1,0:T(8,128)}), f32[32,8,512]{2,1,0:T(8,128)S(1)}, u32[]{:S(2)}, u32[]{:S(2)}) async-start(f32[32,8,512]{2,1,0:T(8,128)} %broadcast_in_dim.27), calls=%async_computation.4 | async-start | bytes 1048576 | tf_op jit(solution)/shard_map/all_to_all | solution.py:178
  137.1 6.5 %collective-permute-start.10 = (f32[256,512]{1,0:T(8,128)S(1)}, f32[256,512]{1,0:T(8,128)S(1)}, u32[]{:S(2)}, u32[]{:S(2)}) collective-permute-start(f32[256,512]{1,0:T(8,128)S(1)} %bitcast.19), channel_id=1, source_target_pairs={{0,8},{8,0},{1,9},{9,1},{2,10},{10,2},{3,11},{11,3},{4,12},{12,4},... | collective-permute-start | bytes 1572872 | tf_op jit(solution)/shard_map/ppermute | solution.py:186

commit v2 on v0

--- a/solution.py
+++ b/solution.py
@@ -201,12 +201,8 @@
     panels = jnp.where(col == 0, matrix, up + down)
     up = lax.ppermute(panels, "col", [(0, 1), (3, 4), (5, 6)])
     down = lax.ppermute(panels, "col", [(0, 7), (3, 2)])
-    gram_part = gram_part.sum(axis=0)
-    copies = [
-        lax.ppermute(gram_part, "col", [(0, k)]) for k in range(1, lax.axis_size("col"))
-    ]
-    gram_part = jnp.where(col == 0, gram_part, sum(copies))
-    own = exchange(spread(gram_part, chips), PLANE)
+    gram_part = exchange(spread(gram_part.sum(axis=0), lax.axis_size("col")), "col")
+    own = exchange(spread(gram_part[0], chips), PLANE)
     panels = jnp.where((col == 0) | (col == 3) | (col == 5), panels, up + down)
     panels = lax.optimization_barrier(panels)
     products = inner(panels, matrix).reshape(2, -1, WIDE)

time: 130 us -> 123 us (0.946)
  waiting for transfers between devices: 26.2 us -> 20.5 us
  starting transfers between devices: 72.2 us -> 69.9 us
    ppermute x7 -> x0, starting transfers between devices: 9.02 us -> none  [steps(): lax.ppermute(gram_part, 'col', [(0, k)])]
    all_to_all x4 -> x5, waiting for transfers between devices: 23.2 us -> 17.5 us  [exchange(): return lax.all_to_all(blocks, axis, 0, 0, tiled=True)]
    all_to_all x4 -> x5, starting transfers between devices: 30.8 us -> 35.8 us  [exchange(): return lax.all_to_all(blocks, axis, 0, 0, tiled=True)]
    ppermute x4, starting transfers between devices: 16.9 us -> 18.6 us  [swapped(): return lax.ppermute(array, 'core', [(0, 1), (1, 0)])]
  transfers between devices with their start and end apart: 19 -> 13, of which waited for: 6 -> 7; matrix products, arithmetic and copies ran while one was open for 5% -> 6% of each run, Pallas kernels for 15% -> 16%
where the time goes in v2:
time: 123 us; the launch traced here: 122 us
  starting transfers between devices  69.9 us (57%)
  waiting for transfers between devices  20.5 us (17%)
  Pallas kernels  19.2 us (16%)
  matrix products  5.94 us (5%)
  local copies, waits for them, and re-layouts  3.33 us (3%)
  other arithmetic  2.25 us (2%)
    all_to_all x5, starting transfers between devices, exchange(): return lax.all_to_all(blocks, axis, 0, 0, tiled=True)  35.8 us
    pallas_call x3, Pallas kernels, call(): pl.pallas_call(kernel, out_shape=[jax.ShapeDtypeStruct(shape, jnp.float32...  19.2 us
    ppermute x4, starting transfers between devices, swapped(): return lax.ppermute(array, 'core', [(0, 1), (1, 0)])  18.6 us
    all_to_all x5, waiting for transfers between devices, exchange(): return lax.all_to_all(blocks, axis, 0, 0, tiled=True)  17.5 us
    ppermute x1, starting transfers between devices, steps(): down = lax.ppermute(matrix, 'col', [(0, 5)])  11.5 us
    dot_general x3, matrix products, product(): jnp.dot(left, right, precision=HIGHEST, preferred_element_type=jnp.float32)  4.91 us
    ppermute x4, waiting for transfers between devices, swapped(): return lax.ppermute(array, 'core', [(0, 1), (1, 0)])  2.94 us
  transfers between devices with their start and end apart: 13, of which 7 were waited for; matrix products, arithmetic and copies ran while one was open for 6% of the time, Pallas kernels for 16%

profile of v2, /device:TPU:1, one launch (start us, length us, event | category | flops | bytes accessed | tf_op | source)
XLA Modules:
  0.0 122.0 jit_solution(17512077474547203264)
XLA Ops:
  0.6 11.5 %collective-permute-start.1 = (f32[256,512]{1,0:T(8,128)}, f32[256,512]{1,0:T(8,128)S(1)}, u32[]{:S(2)}, u32[]{:S(2)}) collective-permute-start(f32[256,512]{1,0:T(8,128)} %panels_ref.1), channel_id=1, source_target_pairs={{0,5},{8,13},{16,21},{24,29},{32,37},{40,45},{48,53},{56,61},{64,6... | collective-permute-start | bytes 1572872 | tf_op jit(solution)/shard_map/ppermute | solution.py:197
  12.1 1.3 %collective-permute-start = (f32[256,512]{1,0:T(8,128)}, f32[256,512]{1,0:T(8,128)S(1)}, u32[]{:S(2)}, u32[]{:S(2)}) collective-permute-start(f32[256,512]{1,0:T(8,128)} %panels_ref.1), channel_id=1, source_target_pairs={{0,3},{8,11},{16,19},{24,27},{32,35},{40,43},{48,51},{56,59},{64,6... | collective-permute-start | bytes 1572872 | tf_op jit(solution)/shard_map/ppermute | solution.py:196
  13.5 0.0 copy-start
  13.5 1.0 copy-done
  14.5 1.7 %shard_map.30 = (f32[32,4,640]{2,1,0:T(4,128)S(1)}, f32[32,4,640]{2,1,0:T(4,128)S(1)}) custom-call(s32[1]{0:T(128)} %bitcast.core_ref, f32[256,512]{1,0:T(8,128)S(1)} %copy-done), custom_call_target="tpu_custom_call" | custom-call | flops 600000000 | bytes 2097152 | tf_op jit(solution)/shard_map/pallas_call | solution.py:167
  16.2 2.9 %collective-permute-start.5 = (f32[32,4,640]{2,1,0:T(4,128)S(1)}, f32[32,4,640]{2,1,0:T(4,128)S(1)}, u32[]{:S(2)}, u32[]{:S(2)}) collective-permute-start(f32[32,4,640]{2,1,0:T(4,128)S(1)} %get-tuple-element.11), channel_id=1, source_target_pairs={{0,8},{8,0},{1,9},{9,1},{2,10},{10,2},{3,11},{11,3},{4,12},{12,4},... | collective-permute-start | bytes 983048 | tf_op jit(solution)/shard_map/ppermute | solution.py:186
  19.1 1.2 %collective-permute-done.5 = f32[32,4,640]{2,1,0:T(4,128)S(1)} collective-permute-done((f32[32,4,640]{2,1,0:T(4,128)S(1)}, f32[32,4,640]{2,1,0:T(4,128)S(1)}, u32[]{:S(2)}, u32[]{:S(2)}) %collective-permute-start.5) | collective-permute-done | bytes 327712 | tf_op jit(solution)/shard_map/ppermute | solution.py:186
  20.3 0.8 add.18
  21.2 0.0 copy-start.1
  21.2 9.8 %all-to-all-start = ((f32[32,4,640]{2,1,0:T(4,128)}), f32[32,4,640]{2,1,0:T(4,128)S(1)}, u32[]{:S(2)}, u32[]{:S(2)}) async-start(f32[32,4,640]{2,1,0:T(4,128)} %add.18), calls=%async_computation | async-start | bytes 655360 | tf_op jit(solution)/shard_map/all_to_all | solution.py:178
  31.0 0.0 collective-permute-done.1
  31.0 0.0 collective-permute-done
  31.0 0.0 copy-done.1
  31.0 0.1 add_select_fusion.1
  31.2 1.3 %collective-permute-start.3 = (f32[256,512]{1,0:T(8,128)S(1)}, f32[256,512]{1,0:T(8,128)S(1)}, u32[]{:S(2)}, u32[]{:S(2)}) collective-permute-start(f32[256,512]{1,0:T(8,128)S(1)} %add_select_fusion.1), channel_id=1, source_target_pairs={{0,7},{3,2},{8,15},{11,10},{16,23},{19,18},{24,31},{27,26},{32,39}... | collective-permute-start | bytes 1572872 | tf_op jit(solution)/shard_map/ppermute | solution.py:203
  32.5 1.3 %collective-permute-start.2 = (f32[256,512]{1,0:T(8,128)S(1)}, f32[256,512]{1,0:T(8,128)S(1)}, u32[]{:S(2)}, u32[]{:S(2)}) collective-permute-start(f32[256,512]{1,0:T(8,128)S(1)} %add_select_fusion.1), channel_id=1, source_target_pairs={{0,1},{3,4},{5,6},{8,9},{11,12},{13,14},{16,17},{19,20},{21,22},{2... | collective-permute-start | bytes 1572872 | tf_op jit(solution)/shard_map/ppermute | solution.py:202
  33.8 7.6 %all-to-all-done = f32[32,4,640]{2,1,0:T(4,128)S(1)} async-done(((f32[32,4,640]{2,1,0:T(4,128)}), f32[32,4,640]{2,1,0:T(4,128)S(1)}, u32[]{:S(2)}, u32[]{:S(2)}) %all-to-all-start) | async-done | bytes 327712 | tf_op jit(solution)/shard_map/all_to_all | solution.py:178
  41.5 0.1 reduce_sum.18
  41.5 0.6 broadcast_in_dim.24
  42.2 3.4 %all-to-all-start.1 = ((f32[8,4,640]{2,1,0:T(4,128)}), f32[8,4,640]{2,1,0:T(4,128)S(1)}, u32[]{:S(2)}, u32[]{:S(2)}) async-start(f32[8,4,640]{2,1,0:T(4,128)} %broadcast_in_dim.24), calls=%async_computation.1 | async-start | bytes 163840 | tf_op jit(solution)/shard_map/all_to_all | solution.py:178
  45.5 0.0 collective-permute-done.3
  45.6 0.0 collective-permute-done.2
  45.6 0.2 add_select_fusion
  45.7 1.0 fusion.11
  46.8 0.1 slice_select_fusion
  46.9 5.7 %collective-permute-start.4 = (f32[256,512]{1,0:T(8,128)S(1)}, f32[256,512]{1,0:T(8,128)S(1)}, u32[]{:S(2)}, u32[]{:S(2)}) collective-permute-start(f32[256,512]{1,0:T(8,128)S(1)} %slice_select_fusion), channel_id=1, source_target_pairs={{0,8},{8,0},{1,9},{9,1},{2,10},{10,2},{3,11},{11,3},{4,12},{12,4},... | collective-permute-start | bytes 1572872 | tf_op jit(solution)/shard_map/ppermute | solution.py:186
  52.5 0.3 all-to-all-done.1
  52.9 0.8 broadcast_in_dim.26
  53.6 7.5 %all-to-all-start.2 = ((f32[32,4,640]{2,1,0:T(4,128)}), f32[32,4,640]{2,1,0:T(4,128)S(1)}, u32[]{:S(2)}, u32[]{:S(2)}) async-start(f32[32,4,640]{2,1,0:T(4,128)} %broadcast_in_dim.26), calls=%async_computation.2 | async-start | bytes 655360 | tf_op jit(solution)/shard_map/all_to_all | solution.py:178
  61.1 0.0 collective-permute-done.4
  61.2 0.9 select_add_fusion
  62.1 9.0 %all-to-all-done.2.own_ref = f32[32,4,640]{2,1,0:T(4,128)S(1)} async-done(((f32[32,4,640]{2,1,0:T(4,128)}), f32[32,4,640]{2,1,0:T(4,128)S(1)}, u32[]{:S(2)}, u32[]{:S(2)}) %all-to-all-start.2) | async-done | bytes 327712 | tf_op jit(solution)/shard_map/all_to_all | solution.py:178
  71.1 6.0 %all-to-all-start.3 = ((f32[32,8,512]{2,1,0:T(8,128)}), f32[32,8,512]{2,1,0:T(8,128)S(1)}, u32[]{:S(2)}, u32[]{:S(2)}) async-start(f32[32,8,512]{2,1,0:T(8,128)} %bitcast.2), calls=%async_computation.3 | async-start | bytes 1048576 | tf_op jit(solution)/shard_map/all_to_all | solution.py:178
  77.1 5.1 %collective-permute-start.6 = (f32[32,4,640]{2,1,0:T(4,128)S(1)}, f32[32,4,640]{2,1,0:T(4,128)S(1)}, u32[]{:S(2)}, u32[]{:S(2)}) collective-permute-start(f32[32,4,640]{2,1,0:T(4,128)S(1)} %all-to-all-done.2.own_ref), channel_id=1, source_target_pairs={{0,8},{8,0},{1,9},{9,1},{2,10},{10,2},{3,11},{11,3},{4,12},{12,4},... | collective-permute-start | bytes 983048 | tf_op jit(solution)/shard_map/ppermute | solution.py:186
  82.3 1.2 %collective-permute-done.6.other_ref = f32[32,4,640]{2,1,0:T(4,128)S(1)} collective-permute-done((f32[32,4,640]{2,1,0:T(4,128)S(1)}, f32[32,4,640]{2,1,0:T(4,128)S(1)}, u32[]{:S(2)}, u32[]{:S(2)}) %collective-permute-start.6) | collective-permute-done | bytes 327712 | tf_op jit(solution)/shard_map/ppermute | solution.py:186
  83.5 4.9 %shard_map.31.state_ref = f32[512,512]{1,0:T(8,128)S(1)} custom-call(s32[1]{0:T(128)} %bitcast.core_ref, f32[32,4,640]{2,1,0:T(4,128)S(1)} %all-to-all-done.2.own_ref, f32[32,4,640]{2,1,0:T(4,128)S(1)} %collective-permute-done.6.other_ref), custom_call_target="tpu_custom_call" | custom-call | flops 1000000000 | bytes 2097152 | tf_op jit(solution)/shard_map/pallas_call | solution.py:167
  88.5 0.6 all-to-all-done.3
  89.1 0.9 broadcast_in_dim.27
  89.9 9.1 %all-to-all-start.4 = ((f32[32,8,512]{2,1,0:T(8,128)}), f32[32,8,512]{2,1,0:T(8,128)S(1)}, u32[]{:S(2)}, u32[]{:S(2)}) async-start(f32[32,8,512]{2,1,0:T(8,128)} %broadcast_in_dim.27), calls=%async_computation.4 | async-start | bytes 1048576 | tf_op jit(solution)/shard_map/all_to_all | solution.py:178
  99.1 12.6 %shard_map.32 = f32[512,512]{1,0:T(8,128)S(1)} custom-call(f32[512,512]{1,0:T(8,128)S(1)} %shard_map.31.state_ref), custom_call_target="tpu_custom_call" | custom-call | flops 1000000000 | bytes 2097152 | tf_op jit(solution)/shard_map/pallas_call | solution.py:167
  111.6 1.9 %convolution_multiply_fusion = f32[256,512]{1,0:T(8,128)} fusion(f32[256,512]{1,0:T(8,128)S(1)} %add_select_fusion, f32[512,512]{1,0:T(8,128)S(1)} %shard_map.32), kind=kOutput, calls=%fused_computation.2 | convolution fusion | flops 805437440 | bytes 2097152 | tf_op jit(solution)/shard_map/dot_general | solution.py:32
  113.5 0.0 all-to-all-done.4
  113.5 5.0 %collective-permute-start.7 = (f32[256,512]{1,0:T(8,128)S(1)}, f32[256,512]{1,0:T(8,128)S(1)}, u32[]{:S(2)}, u32[]{:S(2)}) collective-permute-start(f32[256,512]{1,0:T(8,128)S(1)} %bitcast.11), channel_id=1, source_target_pairs={{0,8},{8,0},{1,9},{9,1},{2,10},{10,2},{3,11},{11,3},{4,12},{12,4},... | collective-permute-start | bytes 1572872 | tf_op jit(solution)/shard_map/ppermute | solution.py:186
  118.4 1.0 fusion.3
  119.5 0.5 collective-permute-done.7
  120.0 2.0 %fusion = f32[512,512]{1,0:T(8,128)} fusion(f32[512,512]{1,0:T(8,128)S(1)} %fusion.3, f32[256,512]{1,0:T(8,128)S(1)} %collective-permute-done.7, pred[]{:T(512)S(6)} %eq.8, f32[512,512]{1,0:T(8,128)S(1)} %shard_map.32, pred[]{:T(512)S(6)} %eq.18), kind=kOutput, calls=%fused_computation.1 | convolution fusion | flops 806486016 | bytes 3670018 | tf_op jit(solution)/shard_map/dot_general | solution.py:32
  (2 shorter events, 0.0 us)
Async XLA Ops:
  0.6 30.3 %collective-permute-start.1 = (f32[256,512]{1,0:T(8,128)}, f32[256,512]{1,0:T(8,128)S(1)}, u32[]{:S(2)}, u32[]{:S(2)}) collective-permute-start(f32[256,512]{1,0:T(8,128)} %panels_ref.1), channel_id=1, source_target_pairs={{0,5},{8,13},{16,21},{24,29},{32,37},{40,45},{48,53},{56,61},{64,6... | collective-permute-start | bytes 1572872 | tf_op jit(solution)/shard_map/ppermute | solution.py:197
  12.1 18.9 %collective-permute-start = (f32[256,512]{1,0:T(8,128)}, f32[256,512]{1,0:T(8,128)S(1)}, u32[]{:S(2)}, u32[]{:S(2)}) collective-permute-start(f32[256,512]{1,0:T(8,128)} %panels_ref.1), channel_id=1, source_target_pairs={{0,3},{8,11},{16,19},{24,27},{32,35},{40,43},{48,51},{56,59},{64,6... | collective-permute-start | bytes 1572872 | tf_op jit(solution)/shard_map/ppermute | solution.py:196
  13.5 1.1 copy-start
  16.2 4.1 %collective-permute-start.5 = (f32[32,4,640]{2,1,0:T(4,128)S(1)}, f32[32,4,640]{2,1,0:T(4,128)S(1)}, u32[]{:S(2)}, u32[]{:S(2)}) collective-permute-start(f32[32,4,640]{2,1,0:T(4,128)S(1)} %get-tuple-element.11), channel_id=1, source_target_pairs={{0,8},{8,0},{1,9},{9,1},{2,10},{10,2},{3,11},{11,3},{4,12},{12,4},... | collective-permute-start | bytes 983048 | tf_op jit(solution)/shard_map/ppermute | solution.py:186
  21.2 9.8 %copy-start.1 = (f32[256,512]{1,0:T(8,128)S(1)}, f32[256,512]{1,0:T(8,128)}, u32[]{:S(2)}) copy-start(f32[256,512]{1,0:T(8,128)} %panels_ref.1) | copy-start | bytes 1572868
  21.2 20.3 %all-to-all-start = ((f32[32,4,640]{2,1,0:T(4,128)}), f32[32,4,640]{2,1,0:T(4,128)S(1)}, u32[]{:S(2)}, u32[]{:S(2)}) async-start(f32[32,4,640]{2,1,0:T(4,128)} %add.18), calls=%async_computation | async-start | bytes 655360 | tf_op jit(solution)/shard_map/all_to_all | solution.py:178
  31.2 14.4 %collective-permute-start.3 = (f32[256,512]{1,0:T(8,128)S(1)}, f32[256,512]{1,0:T(8,128)S(1)}, u32[]{:S(2)}, u32[]{:S(2)}) collective-permute-start(f32[256,512]{1,0:T(8,128)S(1)} %add_select_fusion.1), channel_id=1, source_target_pairs={{0,7},{3,2},{8,15},{11,10},{16,23},{19,18},{24,31},{27,26},{32,39}... | collective-permute-start | bytes 1572872 | tf_op jit(solution)/shard_map/ppermute | solution.py:203
  32.5 13.1 %collective-permute-start.2 = (f32[256,512]{1,0:T(8,128)S(1)}, f32[256,512]{1,0:T(8,128)S(1)}, u32[]{:S(2)}, u32[]{:S(2)}) collective-permute-start(f32[256,512]{1,0:T(8,128)S(1)} %add_select_fusion.1), channel_id=1, source_target_pairs={{0,1},{3,4},{5,6},{8,9},{11,12},{13,14},{16,17},{19,20},{21,22},{2... | collective-permute-start | bytes 1572872 | tf_op jit(solution)/shard_map/ppermute | solution.py:202
  42.2 10.7 %all-to-all-start.1 = ((f32[8,4,640]{2,1,0:T(4,128)}), f32[8,4,640]{2,1,0:T(4,128)S(1)}, u32[]{:S(2)}, u32[]{:S(2)}) async-start(f32[8,4,640]{2,1,0:T(4,128)} %broadcast_in_dim.24), calls=%async_computation.1 | async-start | bytes 163840 | tf_op jit(solution)/shard_map/all_to_all | solution.py:178
  46.9 14.3 %collective-permute-start.4 = (f32[256,512]{1,0:T(8,128)S(1)}, f32[256,512]{1,0:T(8,128)S(1)}, u32[]{:S(2)}, u32[]{:S(2)}) collective-permute-start(f32[256,512]{1,0:T(8,128)S(1)} %slice_select_fusion), channel_id=1, source_target_pairs={{0,8},{8,0},{1,9},{9,1},{2,10},{10,2},{3,11},{11,3},{4,12},{12,4},... | collective-permute-start | bytes 1572872 | tf_op jit(solution)/shard_map/ppermute | solution.py:186
  53.6 17.4 %all-to-all-start.2 = ((f32[32,4,640]{2,1,0:T(4,128)}), f32[32,4,640]{2,1,0:T(4,128)S(1)}, u32[]{:S(2)}, u32[]{:S(2)}) async-start(f32[32,4,640]{2,1,0:T(4,128)} %broadcast_in_dim.26), calls=%async_computation.2 | async-start | bytes 655360 | tf_op jit(solution)/shard_map/all_to_all | solution.py:178
  71.1 17.9 %all-to-all-start.3 = ((f32[32,8,512]{2,1,0:T(8,128)}), f32[32,8,512]{2,1,0:T(8,128)S(1)}, u32[]{:S(2)}, u32[]{:S(2)}) async-start(f32[32,8,512]{2,1,0:T(8,128)} %bitcast.2), calls=%async_computation.3 | async-start | bytes 1048576 | tf_op jit(solution)/shard_map/all_to_all | solution.py:178
  77.1 6.4 %collective-permute-start.6 = (f32[32,4,640]{2,1,0:T(4,128)S(1)}, f32[32,4,640]{2,1,0:T(4,128)S(1)}, u32[]{:S(2)}, u32[]{:S(2)}) collective-permute-start(f32[32,4,640]{2,1,0:T(4,128)S(1)} %all-to-all-done.2.own_ref), channel_id=1, source_target_pairs={{0,8},{8,0},{1,9},{9,1},{2,10},{10,2},{3,11},{11,3},{4,12},{12,4},... | collective-permute-start | bytes 983048 | tf_op jit(solution)/shard_map/ppermute | solution.py:186
  89.9 23.6 %all-to-all-start.4 = ((f32[32,8,512]{2,1,0:T(8,128)}), f32[32,8,512]{2,1,0:T(8,128)S(1)}, u32[]{:S(2)}, u32[]{:S(2)}) async-start(f32[32,8,512]{2,1,0:T(8,128)} %broadcast_in_dim.27), calls=%async_computation.4 | async-start | bytes 1048576 | tf_op jit(solution)/shard_map/all_to_all | solution.py:178
  113.5 6.5 %collective-permute-start.7 = (f32[256,512]{1,0:T(8,128)S(1)}, f32[256,512]{1,0:T(8,128)S(1)}, u32[]{:S(2)}, u32[]{:S(2)}) collective-permute-start(f32[256,512]{1,0:T(8,128)S(1)} %bitcast.11), channel_id=1, source_target_pairs={{0,8},{8,0},{1,9},{9,1},{2,10},{10,2},{3,11},{11,3},{4,12},{12,4},... | collective-permute-start | bytes 1572872 | tf_op jit(solution)/shard_map/ppermute | solution.py:186
